TPU v7x, 32 devices: a whole 2x2x4 slice. The times are simulated.
32 devices in a mesh: blk: 16 (over z, y, x), grp: 2 (over core).
Axes of the slice: x: 2, y: 2, z: 4, core: 2. Of those that a mesh axis runs over, the one named last changes fastest.
Arguments:
- returns: float32 [512, 8192], P(None, ('blk', 'grp')), may hold values from -200 to 200
Outputs:
- correlation: bfloat16 [8192, 8192], P(('blk', 'grp'))
All inputs are finite; a program needn't handle non-finite values.
Results may differ from a plain program's by a relative error of at most 0.0034.
Values may be sent and summed in bfloat16 or wider, within the bound.
A program may use at most 128 MiB of HBM per device.

v0:
```python
import math

import jax
import jax.numpy as jnp
from jax import lax
from jax.sharding import PartitionSpec as P


def gram_tile(first, second):
    return lax.dot_general(
        first, second, (((0,), (0,)), ((), ())), preferred_element_type=jnp.float32
    )


def shards(returns):
    bar_count = returns.shape[0]
    series_dev = returns.shape[1]
    devices = lax.axis_size(("blk", "grp"))
    my_index = lax.axis_index(("blk", "grp"))
    summed = lax.psum(jnp.sum(returns, axis=1), ("blk", "grp"))
    market = summed / (series_dev * devices)
    excess = returns - market[:, None]
    deviation = excess - jnp.mean(excess, axis=0, keepdims=True)
    inverse = lax.rsqrt(jnp.mean(deviation * deviation, axis=0, keepdims=True) + 1e-06) / math.sqrt(
        bar_count
    )
    zscores = (deviation * inverse).astype(jnp.bfloat16)
    piece = lax.all_gather(zscores, ("blk", "grp"), axis=1, tiled=True)
    products = gram_tile(zscores, piece)
    column_block = jnp.arange(piece.shape[1], dtype=jnp.int32) // series_dev
    return jnp.where(column_block[None, :] >= my_index, products, jnp.float32(0.0)).astype(
        jnp.bfloat16
    )


def solution(mesh):
    in_specs = (P(None, ("blk", "grp")),)
    out_specs = P(("blk", "grp"), None)
    return jax.shard_map(shards, mesh=mesh, in_specs=in_specs, out_specs=out_specs, check_vma=False)
```

profile of v0, /device:TPU:0, one launch (start us, length us, event | category | flops | bytes accessed | tf_op | source)
XLA Modules:
  0.0 158.5 jit_solution(11532635164527842564)
XLA Ops:
  6.5 0.0 all-gather.2.cloned.1.call-start
  6.5 1.2 reduce_sum.27
  7.7 42.0 %psum.7 = f32[512]{0:T(512)S(1)} all-reduce(f32[512]{0:T(512)S(1)} %reduce_sum.27), channel_id=1, replica_groups=mesh['blk'=16,'grp'=2] {'blk','grp'}, use_global_device_ids=true, to_apply=%region_1.0 | all-reduce | flops 512 | bytes 4096 | tf_op jit(solution)/shard_map/psum | solution.py:20
  49.7 1.2 subtract_reduce_fusion
  50.9 1.2 multiply_reduce_fusion
  52.1 1.9 %multiply_convert_fusion = bf16[512,256]{1,0:T(8,128)(2,1)} fusion(f32[512,256]{1,0:T(8,128)} %param.1, f32[256]{0:T(256)S(1)} %rsqrt_multiply_fusion, f32[256]{0:T(256)S(1)} %broadcast_multiply_fusion.1, f32[512]{0:T(512)S(1)} %broadcast_multiply_fusion), kind=kLoop, calls=%fused_computation.2 | loop fusion | flops 524288 | bytes 790528 | tf_op jit(solution)/shard_map/convert_element_type | solution.py:27
  54.0 0.0 all-gather.2.cloned.1.call-update
  54.1 89.7 %all-gather.2.cloned.1.call-done = bf16[512,8192]{1,0:T(8,128)(2,1)} async-done(((bf16[512,256]{1,0:T(8,128)(2,1)}), bf16[512,8192]{1,0:T(8,128)(2,1)}) %all-gather.2.cloned.1.call-update) | async-done | bytes 8388624 | tf_op jit(solution)/shard_map/all_gather | solution.py:28
  143.7 7.9 %fusion = bf16[256,8192]{1,0:T(8,128)(2,1)} fusion(bf16[512,256]{1,0:T(8,128)(2,1)} %multiply_convert_fusion, bf16[512,8192]{1,0:T(8,128)(2,1)} %all-gather.2.cloned.1.call-done, pred[8192]{0:T(1024)(128)(4,1)S(1)} %fusion.1), kind=kOutput, calls=%fused_computation.1 | convolution fusion | flops 2151677952 | bytes 12853248 | tf_op jit(solution)/shard_map/dot_general | solution.py:10
  (4 shorter events, 0.0 us)
Async XLA Ops:
  6.5 137.2 %all-gather.2.cloned.1.call-start = ((), (), s32[]{:S(2)}) async-start(), calls=%async_computation | async-start | bytes 8650752 | tf_op jit(solution)/shard_map/all_gather | solution.py:28
Sparse Core Ops, SparseCore 0:
  54.2 89.5 all-gather.1
where the time goes:
time: 159 us; the launch traced here: 158 us
  waiting for transfers between devices  89.7 us (56%)
  blocking collectives  42 us (26%)
  between operations  13.4 us (8%)
  matrix products  7.89 us (5%)
  other arithmetic  5.49 us (3%)
    all_gather x1, waiting for transfers between devices, shards(): piece = lax.all_gather(zscores, ('blk', 'grp'), axis=1, tiled=True)  89.7 us
    psum x1, blocking collectives, shards(): summed = lax.psum(jnp.sum(returns, axis=1), ('blk', 'grp'))  42 us
    dot_general x1, matrix products, gram_tile(): lax.dot_general(first, second, (((0,), (0,)), ((), ())), preferred_elemen...  7.89 us
  transfers between devices with their start and end apart: 1, of which 1 were waited for; matrix products, arithmetic and copies ran while one was open for 0% of the time, Pallas kernels for 0%

commit v1 on v0

v1 whole, which is shorter than its diff:
```python
import functools
import math

import jax
import jax.numpy as jnp
from jax import lax
from jax.experimental import pallas as pl
from jax.experimental.pallas import tpu as pltpu
from jax.sharding import PartitionSpec as P

MESH = pl.DeviceIdType.MESH
ZC, ZX, ZY, ZD, XC, YC, D0, D1, PC = range(9)
KINDS = 12


def kernel(
    planes, r_hbm, out_hbm, r_ref, gath, zt, res, parts, sums, load_sem, out_sem, psend, precv, zsend, zrecv, send, recv
):
    bars, width = r_ref.shape
    series = width * gath.shape[0]
    blk, core = lax.axis_index("blk"), lax.axis_index("grp")
    x, y, z = lax.rem(blk, 2), lax.rem(lax.div(blk, 2), 2), lax.div(blk, 4)
    nx, ny, nc = 1 - x, 1 - y, 1 - core

    def device(zz, yy, xx, cc):
        return {"blk": (zz * 2 + yy) * 2 + xx, "grp": cc}

    def slot(zz, yy, xx, cc):
        return ((zz * 2 + yy) * 2 + xx) * 2 + cc

    mates = [
        device(z, ny if j & 2 else y, nx if j & 1 else x, nc if j & 4 else core) for j in range(1, 8)
    ]
    column = [device(lax.rem(z + d, planes), y, x, core) for d in range(1, planes)]
    barrier = pltpu.get_barrier_semaphore()
    for other in mates + column:
        pl.semaphore_signal(barrier, inc=1, device_id=other, device_id_type=MESH)
    load = pltpu.make_async_copy(r_hbm, r_ref, load_sem)
    load.start()
    load.wait()

    lanes = r_ref[:, :128]
    for i in range(1, width // 128):
        lanes = lanes + r_ref[:, 128 * i : 128 * (i + 1)]
    mine = slot(0, y, x, core)
    parts[mine] = jnp.sum(lanes.T, axis=0, keepdims=True)
    pl.semaphore_wait(barrier, len(mates) + len(column))

    def part_copy(j):
        return pltpu.make_async_remote_copy(
            parts.at[mine], parts.at[mine], psend.at[j], precv.at[j], device_id=mates[j], device_id_type=MESH
        )

    for j in range(7):
        part_copy(j).start()
    for j in range(7):
        part_copy(j).wait_recv()
    sums[z] = jnp.sum(parts[...], axis=0)

    def sum_copy(d):
        return pltpu.make_async_remote_copy(
            sums.at[z], sums.at[z], zsend.at[d], zrecv.at[d], device_id=column[d], device_id_type=MESH
        )

    for d in range(planes - 1):
        sum_copy(d).start()
    for d in range(planes - 1):
        sum_copy(d).wait_recv()
    market = jnp.sum(sums[...], axis=0) * (1.0 / series)
    market = jnp.broadcast_to(market, (128, bars)).T
    own = slot(z, y, x, core)
    for i in range(width // 128):
        excess = r_ref[:, 128 * i : 128 * (i + 1)] - market
        deviation = excess - jnp.mean(excess, axis=0, keepdims=True)
        inverse = lax.rsqrt(jnp.mean(deviation * deviation, axis=0, keepdims=True) + 1e-06) / math.sqrt(bars)
        gath[own, :, 128 * i : 128 * (i + 1)] = (deviation * inverse).astype(jnp.bfloat16)

    split = bars * 25 // 32 // 16 * 16
    half = split // 32 * 16
    whole, first, rest = (0, bars), (0, split), (split, bars - split)

    def copy(block, rows, kind, dz_send, dz_recv, target):
        ref = gath.at[block, pl.ds(*rows)]
        return pltpu.make_async_remote_copy(
            ref, ref, send.at[kind, dz_send], recv.at[kind, dz_recv], device_id=target, device_id_type=MESH
        )

    below, xdev, ydev, partner = device(z - 1, y, x, core), device(z, y, nx, core), device(z, ny, x, core), device(z, y, x, nc)

    class Step:
        def __init__(self, dz):
            self.dz = dz
            self.valid = z + dz < planes
            zz = z + dz
            here = [slot(zz, yy, xx, core) for yy, xx in ((y, x), (y, nx), (ny, x), (ny, nx))]
            there = [slot(zz, yy, xx, nc) for yy, xx in ((y, x), (y, nx), (ny, x), (ny, nx))]
            spread = whole if dz == 0 else first
            cut = bars // 2 if dz == 0 else half
            low, high = (0, cut), (cut, spread[1] - cut)
            to = functools.partial
            self.out = {
                ZC: to(copy, here[0], whole, ZC, dz, dz + 1, below),
                ZX: to(copy, here[1], rest, ZX, dz, dz + 1, below),
                ZY: to(copy, here[2], rest, ZY, dz, dz + 1, below),
                ZD: to(copy, here[3], rest, ZD, dz, dz + 1, below),
                XC: to(copy, here[0], spread, XC, dz, dz, xdev),
                YC: to(copy, here[0], spread, YC, dz, dz, ydev),
                D0: to(copy, here[1], low, D0, dz, dz, ydev),
                D1: to(copy, here[2], high, D1, dz, dz, xdev),
            }
            self.into = {
                ZC: to(copy, here[0], whole, ZC, dz, dz, below),
                ZX: to(copy, here[1], rest, ZX, dz, dz, below),
                ZY: to(copy, here[2], rest, ZY, dz, dz, below),
                ZD: to(copy, here[3], rest, ZD, dz, dz, below),
                XC: to(copy, here[1], spread, XC, dz, dz, xdev),
                YC: to(copy, here[2], spread, YC, dz, dz, ydev),
                D0: to(copy, here[3], low, D0, dz, dz, ydev),
                D1: to(copy, here[3], high, D1, dz, dz, xdev),
            }
            for i in range(4):
                self.out[PC + i] = to(copy, here[i], whole, PC + i, dz, dz, partner)
                self.into[PC + i] = to(copy, there[i], whole, PC + i, dz, dz, partner)

        def start(self, *kinds):
            for kind in kinds:
                if kind in (ZC, ZX, ZY, ZD):
                    if self.dz < planes - 1:
                        pl.when(z > 0)(lambda kind=kind: self.out[kind]().start())
                else:
                    self.out[kind]().start()

        def wait(self, *kinds):
            for kind in kinds:
                self.into[kind]().wait_recv()

        def drain(self):
            for kind, make in self.out.items():
                if kind in (ZC, ZX, ZY, ZD):
                    if self.dz < planes - 1:
                        pl.when(z > 0)(lambda make=make: make().wait_send())
                else:
                    make().wait_send()

        def spread(self):
            if self.dz > 0:
                self.wait(ZC)
            self.start(ZC, XC, YC, PC)

        def turn(self):
            self.wait(XC)
            self.start(D0)
            self.wait(YC)
            self.start(D1)
            if self.dz > 0:
                self.wait(ZX, ZY)
            self.start(ZX, ZY, PC + 1, PC + 2)
            if self.dz > 0:
                self.wait(ZD)
                self.start(ZD)

        def corner(self):
            self.wait(D0, D1)
            if self.dz == 0:
                self.start(ZD)
            self.start(PC + 3)

        def multiply(self):
            self.wait(PC, PC + 1, PC + 2, PC + 3)
            base = (z + self.dz) * 8

            @pl.loop(0, 8)
            def _(i):
                at = pl.ds(pl.multiple_of((base + i) * width, width), width)
                res[:, at] = jnp.dot(zt[...], gath[base + i], preferred_element_type=jnp.float32).astype(jnp.bfloat16)

            self.store().start()

        def store(self):
            at = pl.ds(pl.multiple_of((z + self.dz) * 8 * width, 8 * width), 8 * width)
            return pltpu.make_async_copy(res.at[:, at], out_hbm.at[:, at], out_sem.at[self.dz])

    steps = [Step(dz) for dz in range(planes)]

    def stage(dz, name):
        if 0 <= dz < planes:
            if dz == 0:
                getattr(steps[dz], name)()
            else:
                pl.when(steps[dz].valid)(getattr(steps[dz], name))

    for t in range(planes + 3):
        stage(t, "spread")
        if t == 0:
            zt[...] = gath[own].T
        stage(t - 1, "turn")
        stage(t - 2, "corner")
        stage(t - 3, "multiply")
    for j in range(7):
        part_copy(j).wait_send()
    for d in range(planes - 1):
        sum_copy(d).wait_send()
    for dz in range(planes):
        stage(dz, "drain")
        pl.when(steps[dz].valid)(lambda dz=dz: steps[dz].store().wait())


def shards(planes, returns):
    bars, width = returns.shape
    blocks = planes * 8
    products = pl.pallas_call(
        functools.partial(kernel, planes),
        out_shape=jax.ShapeDtypeStruct((width, blocks * width), jnp.bfloat16),
        in_specs=[pl.BlockSpec(memory_space=pl.ANY)],
        out_specs=pl.BlockSpec(memory_space=pl.ANY),
        scratch_shapes=[
            pltpu.VMEM((bars, width), jnp.float32),
            pltpu.VMEM((blocks, bars, width), jnp.bfloat16),
            pltpu.VMEM((width, bars), jnp.bfloat16),
            pltpu.VMEM((width, blocks * width), jnp.bfloat16),
            pltpu.VMEM((8, 1, bars), jnp.float32),
            pltpu.VMEM((planes, 1, bars), jnp.float32),
            pltpu.SemaphoreType.DMA,
            pltpu.SemaphoreType.DMA((planes,)),
            pltpu.SemaphoreType.DMA((7,)),
            pltpu.SemaphoreType.DMA((7,)),
            pltpu.SemaphoreType.DMA((max(planes - 1, 1),)),
            pltpu.SemaphoreType.DMA((max(planes - 1, 1),)),
            pltpu.SemaphoreType.DMA((KINDS, planes)),
            pltpu.SemaphoreType.DMA((KINDS, planes)),
        ],
        compiler_params=pltpu.CompilerParams(collective_id=0, has_side_effects=True),
    )(returns)
    my_index = lax.axis_index(("blk", "grp"))
    column_block = jnp.arange(blocks * width, dtype=jnp.int32) // width
    return jnp.where(column_block[None, :] >= my_index, products, jnp.bfloat16(0.0))


def solution(mesh):
    planes = mesh.shape["blk"] // 4
    in_specs = (P(None, ("blk", "grp")),)
    out_specs = P(("blk", "grp"), None)
    return jax.shard_map(
        functools.partial(shards, planes), mesh=mesh, in_specs=in_specs, out_specs=out_specs, check_vma=False
    )
```

time: 159 us -> 59.2 us (0.37)
  waiting for transfers between devices: 89.7 us -> 0 us
  Pallas kernels: 0 us -> 54.4 us
  blocking collectives: 42 us -> 0 us
  between operations: 13.4 us -> 0.01 us
  matrix products: 7.89 us -> 0 us
    all_gather x1 -> x0, waiting for transfers between devices: 89.7 us -> none  [shards(): piece = lax.all_gather(zscores, ('blk', 'grp'), axis=1, tiled=True)]
    pallas_call x0 -> x1, Pallas kernels: none -> 54.4 us  [shards(): pl.pallas_call(functools.partial(kernel, planes), out_shape=jax.ShapeDtyp...]
    psum x1 -> x0, blocking collectives: 42 us -> none  [shards(): summed = lax.psum(jnp.sum(returns, axis=1), ('blk', 'grp'))]
    dot_general x1 -> x0, matrix products: 7.89 us -> none  [gram_tile(): lax.dot_general(first, second, (((0,), (0,)), ((), ())), preferred_elemen...]
    select_n x0 -> x1, other arithmetic: none -> 4.54 us  [shards(): jnp.where(column_block[None, :] >= my_index, products, jnp.bfloat16(0.0))]
    reduce_sum x3 -> x0, other arithmetic: 3.57 us -> none  [the longest x1 1.19 us: shards(): jnp.mean(deviation * deviation, axis=0, keepdims=True) + 1e-06]
    convert_element_type x1 -> x0, other arithmetic: 1.9 us -> none  [shards(): zscores = (deviation * inverse).astype(jnp.bfloat16)]
  transfers between devices with their start and end apart: 1 -> 0, of which waited for: 1 -> 0; matrix products, arithmetic and copies ran while one was open for 0% -> 0% of each run, Pallas kernels for 0% -> 0%
where the time goes in v1:
time: 59.2 us; the launch traced here: 59 us
  Pallas kernels  54.4 us (92%)
  other arithmetic  4.55 us (8%)
    pallas_call x1, Pallas kernels, shards(): pl.pallas_call(functools.partial(kernel, planes), out_shape=jax.ShapeDtyp...  54.4 us
    select_n x1, other arithmetic, shards(): jnp.where(column_block[None, :] >= my_index, products, jnp.bfloat16(0.0))  4.54 us

profile of v1, /device:TPU:0, one launch (start us, length us, event | category | flops | bytes accessed | tf_op | source)
XLA Modules:
  0.0 59.0 jit_solution(3050843676124624941)
XLA Ops:
  0.0 54.4 %shard_map.17 = bf16[256,8192]{1,0:T(8,128)(2,1)} custom-call(f32[512,256]{1,0:T(8,128)} %r_hbm.1), custom_call_target="tpu_custom_call" | custom-call | tf_op jit(solution)/shard_map/pallas_call | solution.py:211
  54.4 4.5 %broadcast_select_fusion = bf16[256,8192]{1,0:T(8,128)(2,1)} fusion(bf16[256,8192]{1,0:T(8,128)(2,1)} %shard_map.17, pred[8192]{0:T(1024)(128)(4,1)S(1)} %fusion), kind=kLoop, calls=%fused_computation | loop fusion | flops 2097152 | bytes 8396800 | tf_op jit(solution)/shard_map/jit(_where)/select_n | solution.py:236
  (1 shorter events, 0.0 us)

commit v2 on v0

v2 whole, which is shorter than its diff:
```python
import functools
import math

import jax
import jax.numpy as jnp
from jax import lax
from jax.experimental import pallas as pl
from jax.experimental.pallas import tpu as pltpu
from jax.sharding import PartitionSpec as P

MESH = pl.DeviceIdType.MESH
DOWN = ("ZA", "ZB", "ZO", "ZX", "ZY", "ZD")
SPREAD = ("XA", "XB", "YA", "YB", "D0", "D1")
REST = ("XR", "YR")
PARTNER = ("P0", "P1", "P2", "P3")
KINDS = DOWN + SPREAD + REST + PARTNER
WAITS = {
    "ZA": -0.99, "ZB": -0.69, "ZO": 1.78, "ZX": 1.11, "ZY": 0.89, "ZD": 2.22, "XA": 0.73, "XB": 1.51,
    "YA": 1.22, "YB": 0.52, "XR": 1.64, "YR": 0.76, "D0": 2.25, "D1": 2.77, "M0": 2.85, "M1": 3.16,
}
SENDS = (
    "D1", "XA", "ZA", "P3", "ZD", "YB", "XR", "ZB", "ZX", "D0", "ZY", "P0", "ZO", "YR", "P2", "YA", "P1", "XB",
)


def needs(kind, d):
    first = d == 0
    return {
        "ZA": [] if first else ["ZA"],
        "ZB": [] if first else ["ZB"],
        "ZO": [] if first else ["ZO"],
        "ZX": ["XR"] if first else ["ZX"],
        "ZY": ["YR"] if first else ["ZY"],
        "ZD": ["D1"] if first else ["ZD"],
        "XA": [] if first else ["ZA"],
        "YA": [] if first else ["ZA"],
        "XB": [] if first else ["ZB"],
        "YB": [] if first else ["ZB"],
        "XR": [],
        "YR": [],
        "D0": ["XA"],
        "D1": ["YB", "YR"] if first else ["YB"],
        "P0": [] if first else ["ZA", "ZB", "ZO"],
        "P1": ["XA", "XB", "XR" if first else "ZX"],
        "P2": ["YA", "YB", "YR" if first else "ZY"],
        "P3": ["D0", "D1"] if first else ["D0", "D1", "ZD"],
    }[kind]


def sends_down(action, kind, d):
    return kind in DOWN and action in ("start", "drain")


def plan(planes):
    events = []
    for d in range(planes):
        kinds = SPREAD + (DOWN if d else REST) + ("M0", "M1")
        events += [(d + WAITS[kind], kind, d) for kind in kinds]
    here, sent, actions = set(), set(), []

    def send():
        for d in range(planes):
            for kind in SENDS:
                absent = (kind in REST and d > 0) or (kind in DOWN and d == planes - 1)
                if (kind, d) not in sent and not absent and all((k, d) in here for k in needs(kind, d)):
                    sent.add((kind, d))
                    actions.append(("start", kind, d))

    send()
    for _, kind, d in sorted(events):
        if kind in ("M0", "M1"):
            actions.extend(("wait", k, d) for k in (PARTNER[:3] if kind == "M0" else PARTNER[3:]))
            actions.append(("multiply", kind, d))
        else:
            actions.append(("wait", kind, d))
            here.add((kind, d))
            send()
    return actions


def kernel(
    planes, r_hbm, out_ref, r_ref, gath, zt, parts, sums, load_sem, psend, precv, zsend, zrecv, send, recv
):
    bars, width = r_ref.shape
    series = width * gath.shape[0]
    blk, core = lax.axis_index("blk"), lax.axis_index("grp")
    x, y, z = lax.rem(blk, 2), lax.rem(lax.div(blk, 2), 2), lax.div(blk, 4)
    nx, ny, nc = 1 - x, 1 - y, 1 - core

    def device(zz, yy, xx, cc):
        return {"blk": (zz * 2 + yy) * 2 + xx, "grp": cc}

    def slot(zz, yy, xx, cc):
        return ((zz * 2 + yy) * 2 + xx) * 2 + cc

    mates = [
        device(z, ny if j & 2 else y, nx if j & 1 else x, nc if j & 4 else core) for j in range(1, 8)
    ]
    column = [device(lax.rem(z + d, planes), y, x, core) for d in range(1, planes)]
    barrier = pltpu.get_barrier_semaphore()
    for other in mates + column:
        pl.semaphore_signal(barrier, inc=1, device_id=other, device_id_type=MESH)
    load = pltpu.make_async_copy(r_hbm, r_ref, load_sem)
    load.start()
    load.wait()

    lanes = r_ref[:, :128]
    for i in range(1, width // 128):
        lanes = lanes + r_ref[:, 128 * i : 128 * (i + 1)]
    mine = slot(0, y, x, core)
    parts[mine] = jnp.sum(lanes.T, axis=0, keepdims=True)
    pl.semaphore_wait(barrier, len(mates) + len(column))

    def part_copy(j):
        return pltpu.make_async_remote_copy(
            parts.at[mine], parts.at[mine], psend.at[j], precv.at[j], device_id=mates[j], device_id_type=MESH
        )

    for j in range(7):
        part_copy(j).start()
    for j in range(7):
        part_copy(j).wait_recv()
    sums[z] = jnp.sum(parts[...], axis=0)

    def sum_copy(d):
        return pltpu.make_async_remote_copy(
            sums.at[z], sums.at[z], zsend.at[d], zrecv.at[d], device_id=column[d], device_id_type=MESH
        )

    for d in range(planes - 1):
        sum_copy(d).start()
    for d in range(planes - 1):
        sum_copy(d).wait_recv()
    market = jnp.sum(sums[...], axis=0) * (1.0 / series)
    market = jnp.broadcast_to(market, (128, bars)).T
    own = slot(z, y, x, core)
    for i in range(width // 128):
        excess = r_ref[:, 128 * i : 128 * (i + 1)] - market
        deviation = excess - jnp.mean(excess, axis=0, keepdims=True)
        inverse = lax.rsqrt(jnp.mean(deviation * deviation, axis=0, keepdims=True) + 1e-06) / math.sqrt(bars)
        gath[own, :, 128 * i : 128 * (i + 1)] = (deviation * inverse).astype(jnp.bfloat16)

    high = bars * 25 // 32 // 16 * 16
    half = bars * 13 // 32 // 16 * 16
    rows_a, rows_b, rows_r = (0, half), (half, high - half), (high, bars - high)

    def copy(kind, d, arriving):
        zz = z + d
        link = kind[0] if kind[0] != "D" else ("Y" if kind == "D0" else "X")
        down = link == "Z"
        if arriving:
            flip = {"X": (0, 1), "Y": (1, 0), "D": (1, 1)}.get(kind[0], (0, 0))
        else:
            flip = {"D0": (0, 1), "D1": (1, 0)}.get(kind, (0, 0))
        if down:
            flip = {"ZX": (0, 1), "ZY": (1, 0), "ZD": (1, 1)}.get(kind, (0, 0))
            rows = {"ZA": rows_a, "ZB": rows_b}.get(kind, rows_r)
        elif link == "P":
            flip = {"P0": (0, 0), "P1": (0, 1), "P2": (1, 0), "P3": (1, 1)}[kind]
            rows = (0, bars)
        else:
            last = (half, bars - half) if d == 0 else rows_b
            rows = {"A": rows_a, "B": rows_b, "R": rows_r, "0": rows_a, "1": last}[kind[1]]
        owner = nc if link == "P" and arriving else core
        block = slot(zz, ny if flip[0] else y, nx if flip[1] else x, owner)
        target = {
            "Z": device(z - 1, y, x, core),
            "X": device(z, y, nx, core),
            "Y": device(z, ny, x, core),
            "P": device(z, y, x, nc),
        }[link]
        ref, k = gath.at[block, pl.ds(*rows)], KINDS.index(kind)
        return pltpu.make_async_remote_copy(
            ref,
            ref,
            send.at[k, d],
            recv.at[k, d + 1 if down and not arriving else d],
            device_id=target,
            device_id_type=MESH,
        )

    def multiply(kind, d):
        base, count = (0, 6) if kind == "M0" else (6, 2)

        @pl.loop(0, count)
        def _(i):
            chip, other = lax.div(i + base, 2), lax.rem(i, 2)
            flip_x, flip_y = lax.rem(chip, 2), lax.div(chip, 2)
            block = slot(z + d, y + flip_y * (1 - 2 * y), x + flip_x * (1 - 2 * x), other)
            at = pl.ds(pl.multiple_of(block * width, width), width)
            out_ref[:, at] = jnp.dot(zt[...], gath[block], preferred_element_type=jnp.float32).astype(jnp.bfloat16)

    def act(action, kind, d):
        if action == "multiply":
            multiply(kind, d)
        elif action == "wait":
            copy(kind, d, True).wait_recv()
        else:
            end = copy(kind, d, False)
            (end.start if action == "start" else end.wait_send)()

    actions = plan(planes)
    actions += [("drain", kind, d) for action, kind, d in actions if action == "start"]
    transposed = False
    while actions:
        key = (actions[0][2], sends_down(*actions[0]))
        count = 1
        while count < len(actions) and (actions[count][2], sends_down(*actions[count])) == key:
            count += 1
        batch, actions = actions[:count], actions[count:]

        def run(batch=batch):
            for action in batch:
                act(*action)

        if not transposed and batch[0][0] != "start":
            zt[...] = gath[own].T
            transposed = True
        d, down = key
        if down:
            pl.when(jnp.minimum(z, planes - z - d) > 0)(run)
        elif d:
            pl.when(z + d < planes)(run)
        else:
            run()
    for j in range(7):
        part_copy(j).wait_send()
    for d in range(planes - 1):
        sum_copy(d).wait_send()


def shards(planes, returns):
    bars, width = returns.shape
    blocks = planes * 8
    held = blocks * width * (2 * bars + 2 * width) + 6 * bars * width
    products = pl.pallas_call(
        functools.partial(kernel, planes),
        out_shape=jax.ShapeDtypeStruct((width, blocks * width), jnp.bfloat16),
        in_specs=[pl.BlockSpec(memory_space=pltpu.HBM)],
        out_specs=pl.BlockSpec(memory_space=pltpu.VMEM),
        scratch_shapes=[
            pltpu.VMEM((bars, width), jnp.float32),
            pltpu.VMEM((blocks, bars, width), jnp.bfloat16),
            pltpu.VMEM((width, bars), jnp.bfloat16),
            pltpu.VMEM((8, 1, bars), jnp.float32),
            pltpu.VMEM((planes, 1, bars), jnp.float32),
            pltpu.SemaphoreType.DMA,
            pltpu.SemaphoreType.DMA((7,)),
            pltpu.SemaphoreType.DMA((7,)),
            pltpu.SemaphoreType.DMA((max(planes - 1, 1),)),
            pltpu.SemaphoreType.DMA((max(planes - 1, 1),)),
            pltpu.SemaphoreType.DMA((len(KINDS), planes)),
            pltpu.SemaphoreType.DMA((len(KINDS), planes)),
        ],
        compiler_params=pltpu.CompilerParams(
            collective_id=0, has_side_effects=True, vmem_limit_bytes=held + 4 * 1024 * 1024
        ),
    )(returns)
    my_index = lax.axis_index(("blk", "grp"))
    column_block = jnp.arange(blocks * width, dtype=jnp.int32) // width
    return jnp.where(column_block[None, :] >= my_index, products, jnp.bfloat16(0.0))


def solution(mesh):
    planes = mesh.shape["blk"] // 4
    in_specs = (P(None, ("blk", "grp")),)
    out_specs = P(("blk", "grp"), None)
    return jax.shard_map(
        functools.partial(shards, planes), mesh=mesh, in_specs=in_specs, out_specs=out_specs, check_vma=False
    )
```

time: 159 us -> 49.4 us (0.31)
  waiting for transfers between devices: 89.7 us -> 0 us
  Pallas kernels: 0 us -> 45.8 us
  blocking collectives: 42 us -> 0 us
  between operations: 13.4 us -> 0.02 us
  matrix products: 7.89 us -> 0 us
  other arithmetic: 5.49 us -> 2.37 us
    all_gather x1 -> x0, waiting for transfers between devices: 89.7 us -> none  [shards(): piece = lax.all_gather(zscores, ('blk', 'grp'), axis=1, tiled=True)]
    pallas_call x0 -> x1, Pallas kernels: none -> 45.8 us  [shards(): pl.pallas_call(functools.partial(kernel, planes), out_shape=jax.ShapeDtyp...]
    psum x1 -> x0, blocking collectives: 42 us -> none  [shards(): summed = lax.psum(jnp.sum(returns, axis=1), ('blk', 'grp'))]
    dot_general x1 -> x0, matrix products: 7.89 us -> none  [gram_tile(): lax.dot_general(first, second, (((0,), (0,)), ((), ())), preferred_elemen...]
    reduce_sum x3 -> x0, other arithmetic: 3.57 us -> none  [the longest x1 1.19 us: shards(): jnp.mean(deviation * deviation, axis=0, keepdims=True) + 1e-06]
    select_n x0 -> x1, other arithmetic: none -> 2.36 us  [shards(): jnp.where(column_block[None, :] >= my_index, products, jnp.bfloat16(0.0))]
    convert_element_type x1 -> x0, other arithmetic: 1.9 us -> none  [shards(): zscores = (deviation * inverse).astype(jnp.bfloat16)]
  transfers between devices with their start and end apart: 1 -> 0, of which waited for: 1 -> 0; matrix products, arithmetic and copies ran while one was open for 0% -> 0% of each run, Pallas kernels for 0% -> 0%
where the time goes in v2:
time: 49.4 us; the launch traced here: 49.3 us
  Pallas kernels  45.8 us (93%)
  other arithmetic  2.37 us (5%)
  local copies, waits for them, and re-layouts  1.04 us (2%)
    pallas_call x1, Pallas kernels, shards(): pl.pallas_call(functools.partial(kernel, planes), out_shape=jax.ShapeDtyp...  45.8 us
    select_n x1, other arithmetic, shards(): jnp.where(column_block[None, :] >= my_index, products, jnp.bfloat16(0.0))  2.36 us
    unnamed x2, local copies, waits for them, and re-layouts  1.04 us

profile of v2, /device:TPU:0, one launch (start us, length us, event | category | flops | bytes accessed | tf_op | source)
XLA Modules:
  0.0 49.3 jit_solution(17662075233941422914)
XLA Ops:
  0.0 0.0 copy-start
  0.0 1.0 %copy-done = f32[512,256]{1,0:T(8,128)S(1)} copy-done((f32[512,256]{1,0:T(8,128)S(1)}, f32[512,256]{1,0:T(8,128)}, u32[]{:S(2)}) %copy-start) | copy-done | bytes 524312
  1.1 45.8 %shard_map.17 = bf16[256,8192]{1,0:T(8,128)(2,1)S(1)} custom-call(f32[512,256]{1,0:T(8,128)S(1)} %copy-done), custom_call_target="tpu_custom_call" | custom-call | tf_op jit(solution)/shard_map/pallas_call | solution.py:236
  46.9 2.4 %broadcast_select_fusion = bf16[256,8192]{1,0:T(8,128)(2,1)} fusion(bf16[256,8192]{1,0:T(8,128)(2,1)S(1)} %shard_map.17, pred[8192]{0:T(1024)(128)(4,1)S(1)} %fusion), kind=kLoop, calls=%fused_computation | loop fusion | flops 2097152 | bytes 8396800 | tf_op jit(solution)/shard_map/jit(_where)/select_n | solution.py:261
  (1 shorter events, 0.0 us)
Async XLA Ops:
  0.0 1.0 %copy-start = (f32[512,256]{1,0:T(8,128)S(1)}, f32[512,256]{1,0:T(8,128)}, u32[]{:S(2)}) copy-start(f32[512,256]{1,0:T(8,128)} %r_hbm.1) | copy-start | bytes 1572868

commit v3 on v2

--- a/solution.py
+++ b/solution.py
@@ -12,14 +12,14 @@
 DOWN = ("ZA", "ZB", "ZO", "ZX", "ZY", "ZD")
 SPREAD = ("XA", "XB", "YA", "YB", "D0", "D1")
 REST = ("XR", "YR")
-PARTNER = ("P0", "P1", "P2", "P3")
+PARTNER = ("P0", "P1", "P2", "P3", "P4")
 KINDS = DOWN + SPREAD + REST + PARTNER
 WAITS = {
     "ZA": -0.99, "ZB": -0.69, "ZO": 1.78, "ZX": 1.11, "ZY": 0.89, "ZD": 2.22, "XA": 0.73, "XB": 1.51,
     "YA": 1.22, "YB": 0.52, "XR": 1.64, "YR": 0.76, "D0": 2.25, "D1": 2.77, "M0": 2.85, "M1": 3.16,
 }
 SENDS = (
-    "D1", "XA", "ZA", "P3", "ZD", "YB", "XR", "ZB", "ZX", "D0", "ZY", "P0", "ZO", "YR", "P2", "YA", "P1", "XB",
+    "D1", "XA", "ZA", "P3", "P4", "ZD", "YB", "XR", "ZB", "ZX", "D0", "ZY", "P0", "ZO", "YR", "P2", "YA", "P1", "XB",
 )
 
 
@@ -43,7 +43,8 @@
         "P0": [] if first else ["ZA", "ZB", "ZO"],
         "P1": ["XA", "XB", "XR" if first else "ZX"],
         "P2": ["YA", "YB", "YR" if first else "ZY"],
-        "P3": ["D0", "D1"] if first else ["D0", "D1", "ZD"],
+        "P3": ["D0"],
+        "P4": ["D1"] if first else ["D1", "ZD"],
     }[kind]
 
 
@@ -156,8 +157,8 @@
             flip = {"ZX": (0, 1), "ZY": (1, 0), "ZD": (1, 1)}.get(kind, (0, 0))
             rows = {"ZA": rows_a, "ZB": rows_b}.get(kind, rows_r)
         elif link == "P":
-            flip = {"P0": (0, 0), "P1": (0, 1), "P2": (1, 0), "P3": (1, 1)}[kind]
-            rows = (0, bars)
+            flip = {"P0": (0, 0), "P1": (0, 1), "P2": (1, 0)}.get(kind, (1, 1))
+            rows = {"P3": rows_a, "P4": (half, bars - half)}.get(kind, (0, bars))
         else:
             last = (half, bars - half) if d == 0 else rows_b
             rows = {"A": rows_a, "B": rows_b, "R": rows_r, "0": rows_a, "1": last}[kind[1]]
@@ -255,7 +256,7 @@
         compiler_params=pltpu.CompilerParams(
             collective_id=0, has_side_effects=True, vmem_limit_bytes=held + 4 * 1024 * 1024
         ),
-    )(returns)
+    )(pltpu.with_memory_space_constraint(returns, pltpu.HBM))
     my_index = lax.axis_index(("blk", "grp"))
     column_block = jnp.arange(blocks * width, dtype=jnp.int32) // width
     return jnp.where(column_block[None, :] >= my_index, products, jnp.bfloat16(0.0))

time: 49.4 us -> 48.7 us (0.986)
  local copies, waits for them, and re-layouts: 1.04 us -> 0 us
    unnamed x2 -> x0, local copies, waits for them, and re-layouts: 1.04 us -> none
where the time goes in v3:
time: 48.7 us; the launch traced here: 48.6 us
  Pallas kernels  46.2 us (95%)
  other arithmetic  2.37 us (5%)
    pallas_call x1, Pallas kernels, shards(): pl.pallas_call(functools.partial(kernel, planes), out_shape=jax.ShapeDtyp...  46.2 us
    select_n x1, other arithmetic, shards(): jnp.where(column_block[None, :] >= my_index, products, jnp.bfloat16(0.0))  2.36 us

profile of v3, /device:TPU:0, one launch (start us, length us, event | category | flops | bytes accessed | tf_op | source)
XLA Modules:
  0.0 48.6 jit_solution(2101962730552304866)
XLA Ops:
  0.0 46.2 %shard_map.17 = bf16[256,8192]{1,0:T(8,128)(2,1)S(1)} custom-call(f32[512,256]{1,0:T(8,128)} %r_hbm.1), custom_call_target="tpu_custom_call" | custom-call | tf_op jit(solution)/shard_map/pallas_call | solution.py:237
  46.2 2.4 %broadcast_select_fusion = bf16[256,8192]{1,0:T(8,128)(2,1)} fusion(bf16[256,8192]{1,0:T(8,128)(2,1)S(1)} %shard_map.17, pred[8192]{0:T(1024)(128)(4,1)S(1)} %fusion), kind=kLoop, calls=%fused_computation | loop fusion | flops 2097152 | bytes 8396800 | tf_op jit(solution)/shard_map/jit(_where)/select_n | solution.py:262
  (1 shorter events, 0.0 us)

commit v4 on v3

--- a/solution.py
+++ b/solution.py
@@ -13,13 +13,30 @@
 SPREAD = ("XA", "XB", "YA", "YB", "D0", "D1")
 REST = ("XR", "YR")
 PARTNER = ("P0", "P1", "P2", "P3", "P4")
+PRODUCTS = ("M0", "M1", "M2", "M3")
 KINDS = DOWN + SPREAD + REST + PARTNER
 WAITS = {
-    "ZA": -0.99, "ZB": -0.69, "ZO": 1.78, "ZX": 1.11, "ZY": 0.89, "ZD": 2.22, "XA": 0.73, "XB": 1.51,
-    "YA": 1.22, "YB": 0.52, "XR": 1.64, "YR": 0.76, "D0": 2.25, "D1": 2.77, "M0": 2.85, "M1": 3.16,
+    "ZA": -0.08,
+    "ZB": 0.26,
+    "ZO": 1.1,
+    "ZX": 2.33,
+    "ZY": 1.62,
+    "ZD": 2.78,
+    "XA": 1.26,
+    "XB": 2.64,
+    "YA": 1.39,
+    "YB": 1.22,
+    "XR": 1.54,
+    "YR": 0.39,
+    "D0": 2.83,
+    "D1": 2.89,
+    "M0": 1.43,
+    "M1": 3.2,
+    "M2": 2.03,
+    "M3": 3.72,
 }
 SENDS = (
-    "D1", "XA", "ZA", "P3", "P4", "ZD", "YB", "XR", "ZB", "ZX", "D0", "ZY", "P0", "ZO", "YR", "P2", "YA", "P1", "XB",
+    "D1", "XA", "YR", "P1", "ZA", "P2", "ZB", "ZX", "P3", "P4", "YB", "XR", "XB", "D0", "ZO", "ZD", "ZY", "P0", "YA",
 )
 
 
@@ -55,7 +72,7 @@
 def plan(planes):
     events = []
     for d in range(planes):
-        kinds = SPREAD + (DOWN if d else REST) + ("M0", "M1")
+        kinds = SPREAD + (DOWN if d else REST) + PRODUCTS
         events += [(d + WAITS[kind], kind, d) for kind in kinds]
     here, sent, actions = set(), set(), []
 
@@ -69,8 +86,8 @@
 
     send()
     for _, kind, d in sorted(events):
-        if kind in ("M0", "M1"):
-            actions.extend(("wait", k, d) for k in (PARTNER[:3] if kind == "M0" else PARTNER[3:]))
+        if kind in PRODUCTS:
+            actions.extend(("wait", k, d) for k in (PARTNER[3:] if kind == "M3" else ("P" + kind[1],)))
             actions.append(("multiply", kind, d))
         else:
             actions.append(("wait", kind, d))
@@ -181,13 +198,11 @@
         )
 
     def multiply(kind, d):
-        base, count = (0, 6) if kind == "M0" else (6, 2)
-
-        @pl.loop(0, count)
-        def _(i):
-            chip, other = lax.div(i + base, 2), lax.rem(i, 2)
-            flip_x, flip_y = lax.rem(chip, 2), lax.div(chip, 2)
-            block = slot(z + d, y + flip_y * (1 - 2 * y), x + flip_x * (1 - 2 * x), other)
+        far_y, far_x = divmod(int(kind[1]), 2)
+
+        @pl.loop(0, 2)
+        def _(other):
+            block = slot(z + d, ny if far_y else y, nx if far_x else x, other)
             at = pl.ds(pl.multiple_of(block * width, width), width)
             out_ref[:, at] = jnp.dot(zt[...], gath[block], preferred_element_type=jnp.float32).astype(jnp.bfloat16)
 

time: 48.7 us -> 49 us (level)
  no operation moved by 1% of the time
where the time goes in v4:
time: 49 us; the launch traced here: 48.4 us
  Pallas kernels  46.1 us (94%)
  other arithmetic  2.37 us (5%)
    pallas_call x1, Pallas kernels, shards(): pl.pallas_call(functools.partial(kernel, planes), out_shape=jax.ShapeDtyp...  46.1 us
    select_n x1, other arithmetic, shards(): jnp.where(column_block[None, :] >= my_index, products, jnp.bfloat16(0.0))  2.36 us

profile of v4, /device:TPU:0, one launch (start us, length us, event | category | flops | bytes accessed | tf_op | source)
XLA Modules:
  0.0 48.4 jit_solution(7177003217040529207)
XLA Ops:
  0.0 46.1 %shard_map.17 = bf16[256,8192]{1,0:T(8,128)(2,1)S(1)} custom-call(f32[512,256]{1,0:T(8,128)} %r_hbm.1), custom_call_target="tpu_custom_call" | custom-call | tf_op jit(solution)/shard_map/pallas_call | solution.py:252
  46.1 2.4 %broadcast_select_fusion = bf16[256,8192]{1,0:T(8,128)(2,1)} fusion(bf16[256,8192]{1,0:T(8,128)(2,1)S(1)} %shard_map.17, pred[8192]{0:T(1024)(128)(4,1)S(1)} %fusion), kind=kLoop, calls=%fused_computation | loop fusion | flops 2097152 | bytes 8396800 | tf_op jit(solution)/shard_map/jit(_where)/select_n | solution.py:277
  (1 shorter events, 0.0 us)
